TPU v7x, 128 devices: a whole 4x4x4 slice. The times are simulated.
128 devices in a mesh: grp: 4 (over z_hi, core), own: 32 (over z_lo, x, y).
Axes of the slice: x: 4, y: 4, z: 4 (z_hi: 2, z_lo: 2; z = z_hi * 2 + z_lo), core: 2. Of those that a mesh axis runs over, the one named last changes fastest.
Arguments:
- features: float32 [131072, 1024], P(('grp', 'own')), may hold values from -9 to 9, as said below
- targets: float32 [131072, 256], P(('grp', 'own')), may hold values from -6 to 6
- centres: float32 [4096, 1024], P('own'), may hold values from -6 to 6
- widths: float32 [4096], P('own'), may hold values from 256 to 1024
- coefficients: float32 [4096, 256], P('own'), may hold values from -0.375 to 0.375
Outputs:
- residual: float32 [131072, 256], P(('grp', 'own'))
- gradient: float32 [4096, 256], P('own')
Inputs may be any that keep to these rules, and one draw needn't show every extreme that they name: Every row of features lies near one of the centres; which centre it is is not promised.
All inputs are finite; a program needn't handle non-finite values.
Results may differ from a plain program's by a relative error of at most 0.00015.
Values sent between devices are 32-bit elements; how exact they have to be, the bound alone decides.
A program may use at most 128 MiB of HBM per device.

v0:
```python
import jax
import jax.numpy as jnp
from jax import lax
from jax.sharding import PartitionSpec as P


def side_by_side(arrays, axis, dim, along):
    columns = [a.reshape(*a.shape[:along], -1) for a in arrays]
    both = jnp.concatenate(columns, axis=along)
    result, at, done = (lax.all_gather(both, axis, axis=dim, tiled=True), 0, [])
    for a, column in zip(arrays, columns):
        section = result[..., at : at + column.shape[along]]
        done.append(section.reshape(*section.shape[:along], *a.shape[along:]))
        at += column.shape[along]
    return tuple(done)


def split_up(x, dim, peers):
    before, after = (x.shape[:dim], x.shape[dim + 1 :])
    return jnp.moveaxis(x.reshape(*before, peers, -1, *after), dim, 0)


def sum_at_owner(x, axis, dim):
    parts = split_up(x, dim, lax.axis_size(axis))
    arrived = lax.all_to_all(parts, axis, split_axis=0, concat_axis=0, tiled=True)
    return arrived.sum(axis=0)


def total_of_pieces(x, axis):
    parts = lax.all_gather(x, axis)
    return parts.sum(axis=0)


def body(features, targets, centres, widths, coefficients):
    row_count = features.shape[0]
    owners = lax.axis_size("own")
    total_rows = row_count * lax.axis_size("grp") * owners
    row_sq = jnp.sum(features * features, axis=1)
    cen_piece, width_piece, coef_piece = side_by_side((centres, widths, coefficients), "own", 0, 1)
    cross = jnp.dot(
        features, cen_piece.T, precision=lax.Precision.HIGHEST, preferred_element_type=jnp.float32
    )
    cen_sq = jnp.sum(cen_piece * cen_piece, axis=1)
    sq_dist = row_sq[:, None] + cen_sq[None, :] - 2.0 * cross
    tile = jnp.exp(-sq_dist / (2.0 * width_piece[None, :]))
    predicted = jnp.dot(
        tile, coef_piece, precision=lax.Precision.HIGHEST, preferred_element_type=jnp.float32
    )
    predicted, kernel = (predicted, tile)
    residual = predicted - targets
    factor = 1.0 / jnp.sqrt(jnp.float32(total_rows))
    share = sum_at_owner(
        lax.dot_general(
            kernel,
            residual,
            (((0,), (0,)), ((), ())),
            precision=lax.Precision.HIGHEST,
            preferred_element_type=jnp.float32,
        )
        * factor,
        "own",
        0,
    )
    gradient = total_of_pieces(share, "grp")
    return (residual, gradient)


def solution(mesh):
    return jax.shard_map(
        body,
        mesh=mesh,
        in_specs=(
            P(("grp", "own"), None),
            P(("grp", "own"), None),
            P("own", None),
            P("own"),
            P("own", None),
        ),
        out_specs=(P(("grp", "own"), None), P("own", None)),
        check_vma=False,
    )
```

profile of v0, /device:TPU:1, one launch (start us, length us, event | category | flops | bytes accessed | tf_op | source)
XLA Modules:
  0.0 460.3 jit_solution(4496257908304564175)
XLA Ops:
  7.2 0.0 all-gather.3.cloned.1.call-start
  7.2 0.8 copy.9
  8.0 2.0 concatenate.3
  10.0 0.0 all-gather.3.cloned.1.call-update
  10.0 2.5 multiply_reduce_fusion.1
  12.6 256.6 %all-gather.3.cloned.1.call-done = f32[4096,1281]{1,0:T(8,128)} async-done(((f32[128,1281]{1,0:T(8,128)}), f32[4096,1281]{1,0:T(8,128)}) %all-gather.3.cloned.1.call-update) | async-done | bytes 20987920 | tf_op jit(solution)/shard_map/all_gather | solution.py:10
  269.1 2.2 fusion.9
  271.3 6.9 %multiply_reduce_fusion = f32[4096]{0:T(1024)S(1)} fusion(f32[4096,1281]{1,0:T(8,128)} %all-gather.3.cloned.1.call-done), kind=kLoop, calls=%fused_computation.4 | loop fusion | flops 8384512 | bytes 16793600 | tf_op jit(solution)/shard_map/reduce_sum | solution.py:43
  278.3 0.0 copy-start.1
  278.3 63.6 %fusion.2 = f32[1024,4096]{0,1:T(8,128)S(1)} fusion(f32[4096]{0:T(1024)S(1)} %fusion.9, f32[4096]{0:T(1024)S(1)} %multiply_reduce_fusion, f32[1024]{0:T(1024)S(1)} %multiply_reduce_fusion.1, f32[1024,1024]{1,0:T(8,128)} %param.5, f32[4096,1281]{1,0:T(8,128)} %all-gather.3.cloned.1.call-done), kind=kOutput, calls=%fused_computation.3 | convolution fusion | flops 51560579072 | bytes 37785600 | tf_op jit(solution)/shard_map/dot_general | solution.py:40
  341.9 0.0 copy-done.1
  341.9 30.5 %fusion.10 = f32[1024,256]{1,0:T(8,128)S(1)} fusion(f32[1024,256]{1,0:T(8,128)S(1)} %copy-done.1, f32[1024,4096]{0,1:T(8,128)S(1)} %fusion.2, f32[4096,1281]{1,0:T(8,128)} %all-gather.3.cloned.1.call-done), kind=kOutput, calls=%fused_computation.13 | convolution fusion | flops 12885164032 | bytes 23068672 | tf_op jit(solution)/shard_map/dot_general | solution.py:46
  372.4 0.0 copy-start
  372.5 14.6 %convolution_multiply_fusion = f32[4096,256]{1,0:T(8,128)S(1)} fusion(f32[1024,4096]{0,1:T(8,128)S(1)} %fusion.2, f32[1024,256]{1,0:T(8,128)S(1)} %fusion.10), kind=kOutput, calls=%fused_computation.7 | convolution fusion | flops 12885950464 | bytes 22020096 | tf_op jit(solution)/shard_map/dot_general | solution.py:53
  387.0 52.6 %all_to_all.5 = f32[32,128,256]{2,1,0:T(8,128)} all-to-all(f32[32,128,256]{2,1,0:T(8,128)S(1)} %bitcast.17), channel_id=1, replica_groups=mesh['grp'=4,'own'=32] {'own'}, dimensions={0} | all-to-all | bytes 8388608 | tf_op jit(solution)/shard_map/all_to_all | solution.py:25
  439.7 2.4 reduce_sum.38
  442.1 0.0 copy-done
  442.1 10.6 %all-gather = f32[512,256]{1,0:T(8,128)S(1)} all-gather(f32[128,256]{1,0:T(8,128)S(1)} %reduce_sum.38), channel_id=2, replica_groups=mesh['grp'=4,'own'=32] {'grp'}, dimensions={0}, use_global_device_ids=true | all-gather | bytes 655360 | tf_op jit(solution)/shard_map/all_gather | solution.py:30
  452.7 0.7 reduce_sum.39
Async XLA Ops:
  7.2 261.9 %all-gather.3.cloned.1.call-start = ((), (), s32[]{:S(2)}) async-start(), calls=%async_computation.1 | async-start | bytes 23789568 | tf_op jit(solution)/shard_map/all_gather | solution.py:10
  278.3 63.6 %copy-start.1 = (f32[1024,256]{1,0:T(8,128)S(1)}, f32[1024,256]{1,0:T(8,128)}, u32[]{:S(2)}) copy-start(f32[1024,256]{1,0:T(8,128)} %param.6) | copy-start | bytes 3145732
  372.4 69.7 %copy-start = (f32[1024,256]{1,0:T(8,128)}, f32[1024,256]{1,0:T(8,128)S(1)}, u32[]{:S(2)}) copy-start(f32[1024,256]{1,0:T(8,128)S(1)} %fusion.10) | copy-start | bytes 3145732
Sparse Core Ops, SparseCore 0:
  10.2 258.8 all-gather.2
where the time goes:
time: 461 us; the launch traced here: 460 us
  waiting for transfers between devices  257 us (56%)
  matrix products  109 us (24%)
  blocking collectives  63.2 us (14%)
  other arithmetic  14.8 us (3%)
  between operations  14.1 us (3%)
    all_gather x1, waiting for transfers between devices, side_by_side(): result, at, done = (lax.all_gather(both, axis, axis=dim, tiled=True), 0, [])  257 us
    dot_general x1, matrix products, body(): jnp.dot(features, cen_piece.T, precision=lax.Precision.HIGHEST, preferred...  63.6 us
    all_to_all x1, blocking collectives, sum_at_owner(): lax.all_to_all(parts, axis, split_axis=0, concat_axis=0, tiled=True)  52.6 us
    dot_general x1, matrix products, body(): jnp.dot(tile, coef_piece, precision=lax.Precision.HIGHEST, preferred_elem...  30.5 us
    dot_general x1, matrix products, body(): lax.dot_general(kernel, residual, (((0,), (0,)), ((), ())), precision=lax...  14.6 us
    all_gather x1, blocking collectives, total_of_pieces(): parts = lax.all_gather(x, axis)  10.6 us
  transfers between devices with their start and end apart: 1, of which 1 were waited for; matrix products, arithmetic and copies ran while one was open for 1% of the time, Pallas kernels for 0%

commit v1 on v0

v1 whole, which is shorter than its diff:
```python
import functools
import math
import jax
import jax.numpy as jnp
from jax import lax
from jax.experimental import pallas as pl
from jax.experimental.pallas import tpu as pltpu
from jax.sharding import PartitionSpec as P

F32, BF16, F8 = jnp.float32, jnp.bfloat16, jnp.float8_e4m3fn
NN = (((1,), (0,)), ((), ()))
NT = (((1,), (1,)), ((), ()))
MESH = pl.DeviceIdType.MESH

PIECE = 32
CHUNK = 256
UNITS = 64
DIRS = ("d1+", "d1-", "d2+", "d2-", "z+", "z-")


def messages():
    out = []

    def add(*m):
        out.append(m)

    for r1 in range(4):
        b = (0, r1, 0)
        if r1 == 0:
            add(0, b, (0, 3, 0), None, "d1+")
            add(0, b, (0, 1, 0), None, "d1-")
        if r1 == 3:
            add(0, b, (0, 2, 0), 0, "d1+")
        if r1 == 1:
            add(0, b, (0, 2, 0), 1, "d1-")
        add(0, b, (0, r1, 3), None, "d2+")
        add(0, b, (0, r1, 1), None, "d2-")
        add(0, (0, r1, 3), (0, r1, 2), 0, "d2+")
        add(0, (0, r1, 1), (0, r1, 2), 1, "d2-")
    for r1 in range(4):
        for r2 in range(4):
            add(0, (0, r1, r2), (1, r1, r2), None, "z+" if (r1 + r2) % 2 == 0 else "z-")
    b = (0, 0, 0)
    add(1, b, (0, 0, 3), None, "d2+")
    add(1, b, (0, 0, 1), None, "d2-")
    add(1, (0, 0, 3), (0, 0, 2), 0, "d2+")
    add(1, (0, 0, 1), (0, 0, 2), 1, "d2-")
    for r2 in range(4):
        add(1, (0, 0, r2), (1, 0, r2), None, "z-" if r2 % 2 == 0 else "z+")
    for rz in range(2):
        for r2 in range(4):
            s = (rz, 0, r2)
            add(1, s, (rz, 3, r2), None, "d1+")
            add(1, s, (rz, 1, r2), None, "d1-")
            add(1, (rz, 3, r2), (rz, 2, r2), 0, "d1+")
            add(1, (rz, 1, r2), (rz, 2, r2), 1, "d1-")
    return out


FIRST = (0, 1, 36, 37, 2, 3, 40, 44, 45, 20)
SCHEDULE = (
    ((0, (15, 16, 17, 32)), (1, (6, 7, 8, 24)), (20, ()), (36, (38, 43, 56, 57)), (37, (39, 41, 48, 49)), (40, (60, 61))),
    (),
    ((2, (4, 23)), (3, (5, 21)), (44, (46,)), (45, (47,))),
    ((6, ()), (15, (11, 12, 28)), (32, ()), (43, (72, 73)), (16, (18, 35))),
    ((17, (19, 33)), (56, (58,)), (57, (59,)), (24, ()), (41, (64, 65))),
    ((7, (9, 27)), (8, (10, 25))),
    ((38, ()), (39, (42, 52, 53))),
    ((48, (50,)), (49, (51,)), (23, ()), (28, ()), (4, ()), (5, (22,))),
    ((60, (62,)), (61, (63,)), (21, ()), (35, ())),
    (),
    ((11, (13, 31)), (12, (14, 29)), (46, ()), (47, ())),
    ((18, ()), (19, (34,)), (33, ()), (42, (68, 69))),
    ((9, ()), (10, (26,))),
    ((72, (74,)), (73, (75,)), (13, ()), (14, (30,)), (58, ()), (59, ()), (27, ())),
    ((31, ()), (64, (66,)), (65, (67,))),
    (),
    ((52, (54,)), (53, (55,)), (25, ()), (50, ()), (51, ())),
    ((29, ()), (62, ()), (63, ())),
    ((68, (70,)), (69, (71,))),
    ((22, ()), (74, ()), (75, ()), (34, ()), (66, ()), (67, ())),
    ((54, ()), (55, ()), (70, ()), (71, ()), (30, ())),
    ((26, ()),),
    (),
    (),
)

STEPS = len(SCHEDULE) // 8 - 1
MSGS = messages()


def unit_order():
    place = {(0, (0, 0, 0)): 0, (1, (0, 0, 0)): 1}
    halves = {}
    for point in SCHEDULE:
        for m, _ in point:
            part, _, dst, half, _ = MSGS[m]
            seen = halves.setdefault((part, dst), set())
            seen.update((0, 1) if half is None else (half,))
            if len(seen) == 2:
                place[(part, dst)] = len(place)
    return place


PLACE = unit_order()
UNIT_AT = {v: k for k, v in PLACE.items()}
LOG2E = 1.4426950408889634
S_HI, S_LO = 4.0, 1024.0
S_K, S_KLO = 16.0, 4096.0
S_C, S_CLO = 64.0, 16384.0
S_R, S_RLO = 0.25, 64.0


def dot(a, b, dims):
    return lax.dot_general(a, b, dims, preferred_element_type=F32)


def split(v):
    hi = v.astype(BF16)
    return hi, v - hi.astype(F32)


def main_kernel(
    feat, targ, cent, wid, coef, resid, grad,
    CB, WV, FS, FH, FX, RS, CH, CX, WH, WX, MB, KH, KX, PRED, TG, PR, RES, RP,
    RTH, RTL, RTR, GT, G0, G1, GO,
    ra0, rb0, sa0, sb0, ta0, tb0, ra1, rb1, sa1, sb1, ta1, tb1,
    in_sem, own_sem, d_send, d_recv, g_send, g_recv, r_send, r_recv, f_send, f_recv, out_sem,
):
    rows, depth = feat.shape
    blocks = depth // 128
    unit_rows = CB.shape[1]
    tile = rows // 2
    wide = TG.shape[1]
    lane_w = wide // 128

    grp, own = lax.axis_index("grp"), lax.axis_index("own")
    core, z_hi = lax.rem(grp, 2), grp // 2
    z, x, y = z_hi * 2 + own // 16, lax.rem(own // 4, 4), lax.rem(own, 4)

    def device(d1=0, d2=0, dz=0, dcore=0):
        nx = lax.rem(x + 4 + d1 * (1 - core) + d2 * core, 4)
        ny = lax.rem(y + 4 + d1 * core + d2 * (1 - core), 4)
        nz = lax.rem(z + 4 + dz, 4)
        nc = lax.rem(core + dcore, 2)
        return ((nz // 2) * 2 + nc, lax.rem(nz, 2) * 16 + nx * 4 + ny)

    near = {
        "d1+": device(d1=1), "d1-": device(d1=-1),
        "d2+": device(d2=1), "d2-": device(d2=-1),
        "z+": device(dz=1), "z-": device(dz=-1),
    }
    sibling = device(dcore=1)
    holders = (sibling, device(dz=2), device(dz=2, dcore=1))

    def remote(src, dst, send, recv, to):
        return pltpu.make_async_remote_copy(
            src_ref=src, dst_ref=dst, send_sem=send, recv_sem=recv, device_id=to, device_id_type=MESH
        )

    loads = []

    def load(src, dst):
        copy = pltpu.make_async_copy(src, dst, in_sem.at[len(loads)])
        copy.start()
        loads.append(copy)
        return copy

    load(wid, WV)
    for p in range(2):
        first = pl.multiple_of((core * 2 + p) * PIECE, PIECE)
        for b in range(blocks):
            load(
                cent.at[pl.ds(first, PIECE), pl.ds(b * 128, 128)],
                CB.at[p, pl.ds(b * PIECE, PIECE), :],
            )
        for b in range(lane_w):
            load(
                coef.at[pl.ds(first, PIECE), pl.ds(b * 128, 128)],
                CB.at[p, pl.ds((blocks + b) * PIECE, PIECE), :],
            )
    feat_in = pltpu.make_async_copy(feat, FS.at[0], own_sem.at[0])
    feat_in.start()
    targ_in = pltpu.make_async_copy(targ, TG, own_sem.at[1])
    targ_in.start()

    barrier = pltpu.get_barrier_semaphore()
    peers = list(near.values()) + list(holders)
    for to in peers:
        pl.semaphore_signal(barrier, inc=1, device_id=to, device_id_type=MESH)
    for copy in loads:
        copy.wait()

    row_i = lax.broadcasted_iota(jnp.int32, (PIECE, 128), 0)
    lane_i = lax.broadcasted_iota(jnp.int32, (PIECE, 128), 1)
    eye = (row_i == lane_i).astype(F32)
    meta_row = lax.broadcasted_iota(jnp.int32, (8, 128), 0)
    for p in range(2):
        sq = jnp.zeros((PIECE, 128), F32)
        for b in range(blocks):
            v = CB[p, b * PIECE : (b + 1) * PIECE, :]
            sq = sq + v * v
        norm = jnp.sum(sq, axis=1, keepdims=True)
        picked = jnp.where(lane_i == row_i + (core * 2 + p) * PIECE, WV[...], 0.0)
        width = jnp.sum(picked, axis=1, keepdims=True)
        scale = (-0.5 * LOG2E) / width
        norm = jnp.sum(norm * eye, axis=0, keepdims=True)
        scale = jnp.sum(scale * eye, axis=0, keepdims=True)
        CB[p, unit_rows - 8 : unit_rows, :] = jnp.where(
            meta_row == 0, scale, jnp.where(meta_row == 1, norm, 0.0)
        )
    pl.semaphore_wait(barrier, len(peers))

    cut = (unit_rows // 16) * 8
    spans = {None: (0, unit_rows), 0: (0, cut), 1: (cut, unit_rows - cut)}

    def message(m):
        part, src, dst, half, way = MSGS[m]
        at, size = spans[half]
        return remote(
            CB.at[PLACE[(part, src)], pl.ds(at, size), :],
            CB.at[PLACE[(part, dst)], pl.ds(at, size), :],
            g_send.at[m], g_recv.at[m], near[way],
        )

    def service(point):
        for m, onward in point:
            message(m).wait_recv()
            for n in onward:
                message(n).start()

    for m in FIRST:
        message(m).start()
    feat_out = remote(feat, FS.at[1], d_send.at[0], d_recv.at[0], sibling)
    feat_out.start()

    def prepare_rows(which):
        base = which * rows
        step = min(128, rows)

        @pl.loop(0, rows // step)
        def _(i):
            r = pl.multiple_of(i * step, step)
            v = FS[which, pl.ds(r, step), :]
            hi, lo = split(v)
            to = pl.ds(base + r, step)
            FH[to, :] = hi
            FX[to, 0:depth] = (v * S_HI).astype(F8)
            FX[to, depth : 2 * depth] = (lo * S_LO).astype(F8)
            RS[to, :] = jnp.broadcast_to(jnp.sum(v * v, axis=1, keepdims=True), (step, 128))

    def prepare_chunk(k):
        units = range(8 * k, 8 * k + 8)
        for b in range(blocks):
            v = jnp.concatenate([CB[u, b * PIECE : (b + 1) * PIECE, :] for u in units], axis=0)
            hi, lo = split(v)
            CH[:, b * 128 : (b + 1) * 128] = hi
            CX[:, b * 128 : (b + 1) * 128] = (lo * S_LO).astype(F8)
            CX[:, depth + b * 128 : depth + (b + 1) * 128] = (v * S_HI).astype(F8)
        for b in range(lane_w):
            at = (blocks + b) * PIECE
            v = jnp.concatenate([CB[u, at : at + PIECE, :] for u in units], axis=0)
            hi, lo = split(v)
            WH[:, b * 128 : (b + 1) * 128] = hi
            WX[0:CHUNK, b * 128 : (b + 1) * 128] = (lo * S_CLO).astype(F8)
            WX[CHUNK : 2 * CHUNK, b * 128 : (b + 1) * 128] = (v * S_C).astype(F8)
        for h in range(2):
            total = CB[8 * k + 4 * h, unit_rows - 8 : unit_rows, :]
            for j in range(1, 4):
                meta = CB[8 * k + 4 * h + j, unit_rows - 8 : unit_rows, :]
                total = total + pltpu.roll(meta, j * PIECE, 1)
            MB[:, h * 128 : (h + 1) * 128] = total

    def compute(k, base, n_tiles):
        def tile_body(i):
            r = pl.ds(pl.multiple_of(base + i * tile, tile), tile)
            cross = dot(FH[r, :], CH[...], NT)
            fine = dot(FX[r, :], CX[...], NT)
            norm = RS[r, :]
            norm = jnp.concatenate([norm, norm], axis=1)
            s = (norm + MB[1:2, :]) - 2.0 * cross - fine * (2.0 / (S_HI * S_LO))
            kern = jnp.exp2(s * MB[0:1, :])
            hi, lo = split(kern)
            KH[r, k * CHUNK : (k + 1) * CHUNK] = hi
            both = jnp.concatenate([(kern * S_K).astype(F8), (lo * S_KLO).astype(F8)], axis=1)
            KX[r, 2 * k * CHUNK : 2 * (k + 1) * CHUNK] = both
            term = dot(hi, WH[...], NN) + dot(both, WX[...], NN) * (1.0 / (S_K * S_CLO))
            if k == 0:
                PRED[r, :] = term
            else:
                PRED[r, :] = PRED[r, :] + term

        if n_tiles == 1:
            tile_body(0)
        else:
            pl.loop(0, n_tiles)(tile_body)

    feat_in.wait()
    prepare_rows(0)
    per_step = 4 // STEPS
    pred_out = [
        remote(
            PRED.at[pl.ds(rows + i * tile, tile), :], PR.at[pl.ds(i * tile, tile), :],
            d_send.at[1 + i], d_recv.at[1 + i], sibling,
        )
        for i in range(2)
    ]
    for k in range(8):
        service(SCHEDULE[k * (STEPS + 1)])
        prepare_chunk(k)
        for s in range(STEPS):
            at = s * per_step * tile
            if k == 7:
                at = lax.rem(at + rows, 2 * rows) if not isinstance(at, int) else (at + rows) % (2 * rows)
            if k == 0 and at == rows:
                feat_out.wait_recv()
                prepare_rows(1)
            compute(k, at, per_step)
            if k == 7 and at >= rows:
                for i in range(2):
                    if at <= rows + i * tile < at + per_step * tile:
                        pred_out[i].start()
            service(SCHEDULE[k * (STEPS + 1) + s + 1])

    def factors(v, at):
        t = v.T
        hi, lo = split(t)
        RTH[:, at : at + tile] = hi
        RTL[:, at : at + tile] = (lo * S_RLO).astype(F8)
        RTR[:, at : at + tile] = (t * S_R).astype(F8)

    targ_in.wait()
    res_out = []
    for i in range(2):
        part = pl.ds(i * tile, tile)
        pred_out[i].wait_recv()
        v = PRED[part, :] + PR[part, :] - TG[part, :]
        RES[part, :] = v
        copy = remote(RES.at[part, :], RP.at[part, :], d_send.at[3 + i], d_recv.at[3 + i], sibling)
        copy.start()
        res_out.append(copy)
        factors(v, i * tile)
    resid_out = pltpu.make_async_copy(RES, resid, out_sem.at[0])
    resid_out.start()

    def gradient_term(base, k):
        r = pl.ds(base, rows)
        if isinstance(k, int):
            c0, c1, c2 = k * CHUNK, 2 * k * CHUNK, (2 * k + 1) * CHUNK
        else:
            c0 = pl.multiple_of(k * CHUNK, CHUNK)
            c1 = pl.multiple_of(2 * k * CHUNK, CHUNK)
            c2 = pl.multiple_of((2 * k + 1) * CHUNK, CHUNK)
        term = dot(RTH[:, r], KH[r, pl.ds(c0, CHUNK)], NN)
        fine = dot(RTL[:, r], KX[r, pl.ds(c1, CHUNK)], NN) + dot(RTR[:, r], KX[r, pl.ds(c2, CHUNK)], NN)
        return term + fine * (1.0 / (S_RLO * S_K))

    @pl.loop(0, 8)
    def _(k):
        GT[k] = gradient_term(0, k)

    for i in range(2):
        res_out[i].wait_recv()
        factors(RP[i * tile : (i + 1) * tile, :], rows + i * tile)
    half_piece = PIECE // 2
    for k in range(8):
        t = (GT[k] + gradient_term(rows, k)).T
        for j in range(8):
            part, (rz, r1, r2) = UNIT_AT[8 * k + j]
            for h in range(2):
                at = j * PIECE + h * half_piece
                v = t[at : at + half_piece, :]
                if part == 0:
                    G0[rz, h, r2, r1] = v
                else:
                    G1[r1, r2, rz, h] = v

    sems = [0]

    def copy_of(src, dst, to):
        i = sems[0]
        sems[0] += 1
        return remote(src, dst, r_send.at[i], r_recv.at[i], to)

    sent = []

    class Ring:
        def __init__(self, way, pieces, far, into, a, b):
            up, down = near[way + "+"], near[way + "-"]
            self.into, self.a, self.b = into, a, b
            self.first = [copy_of(far[0], a.at[0], up), copy_of(far[1], a.at[1], down)]
            self.second = [copy_of(pieces[1], b.at[0], up), copy_of(pieces[3], b.at[1], down)]

        def begin(self):
            for c in self.first:
                c.start()

        def middle(self):
            for i in range(2):
                self.first[i].wait_recv()
                ref = self.into[i]
                ref[...] = ref[...] + self.a[i]
                self.second[i].start()

        def end(self, own, out):
            for c in self.second:
                c.wait_recv()
            out[...] = own[...] + self.b[0] + self.b[1]
            sent.extend(self.first + self.second)

    h_here = z_hi
    h_up = lax.rem(z + 1, 4) // 2

    ring0 = Ring(
        "z",
        {1: G0.at[1, h_up], 3: G0.at[1, 1 - h_up]},
        (G0.at[0, 1 - h_here, pl.ds(0, 2)], G0.at[0, 1 - h_here, pl.ds(2, 2)]),
        (G0.at[1, h_up, pl.ds(0, 2)], G0.at[1, 1 - h_up, pl.ds(2, 2)]),
        ra0, rb0,
    )
    ring1 = Ring(
        "d1",
        {1: G1.at[1], 3: G1.at[3]},
        (G1.at[2, pl.ds(0, 2)], G1.at[2, pl.ds(2, 2)]),
        (G1.at[1, pl.ds(0, 2)], G1.at[3, pl.ds(2, 2)]),
        ra1, rb1,
    )
    ring0.begin()
    ring1.begin()
    ring0.middle()
    ring1.middle()
    mine0, mine1 = G0.at[0, h_here], G1.at[0]
    ring1.end(mine1, mine1)
    ring3 = Ring(
        "d2",
        {1: G1.at[0, 1], 3: G1.at[0, 3]},
        (G1.at[0, 2, 0], G1.at[0, 2, 1]),
        (G1.at[0, 1, 0], G1.at[0, 3, 1]),
        sa1, sb1,
    )
    ring3.begin()
    ring0.end(mine0, mine0)
    ring2 = Ring(
        "d2",
        {1: G0.at[0, h_here, 1], 3: G0.at[0, h_here, 3]},
        (G0.at[0, h_here, 2, pl.ds(0, 2)], G0.at[0, h_here, 2, pl.ds(2, 2)]),
        (G0.at[0, h_here, 1, pl.ds(0, 2)], G0.at[0, h_here, 3, pl.ds(2, 2)]),
        sa0, sb0,
    )
    ring2.begin()
    ring3.middle()
    ring2.middle()
    ring3.end(G1.at[0, 0], G1.at[0, 0])
    quarter = half_piece // 2
    ring5 = Ring(
        "z",
        {1: G1.at[0, 0, 1, h_up], 3: G1.at[0, 0, 1, 1 - h_up]},
        (G1.at[0, 0, 0, 1 - h_here, pl.ds(0, quarter)], G1.at[0, 0, 0, 1 - h_here, pl.ds(quarter, quarter)]),
        (G1.at[0, 0, 1, h_up, pl.ds(0, quarter)], G1.at[0, 0, 1, 1 - h_up, pl.ds(quarter, quarter)]),
        ta1, tb1,
    )
    ring5.begin()
    ring2.end(G0.at[0, h_here, 0], G0.at[0, h_here, 0])
    ring4 = Ring(
        "d1",
        {1: G0.at[0, h_here, 0, 1], 3: G0.at[0, h_here, 0, 3]},
        (G0.at[0, h_here, 0, 2, pl.ds(0, quarter)], G0.at[0, h_here, 0, 2, pl.ds(quarter, quarter)]),
        (G0.at[0, h_here, 0, 1, pl.ds(0, quarter)], G0.at[0, h_here, 0, 3, pl.ds(quarter, quarter)]),
        ta0, tb0,
    )
    ring4.begin()
    ring5.middle()
    ring4.middle()

    factor = 1.0 / math.sqrt(TOTAL_ROWS[0])
    ring5.end(G1.at[0, 0, 0, h_here], G1.at[0, 0, 0, h_here])
    ring4.end(G0.at[0, h_here, 0, 0], G0.at[0, h_here, 0, 0])
    last = []
    for p, ref in ((1, G1.at[0, 0, 0, h_here]), (0, G0.at[0, h_here, 0, 0])):
        at = pl.multiple_of((core * 2 + p) * PIECE + z_hi * half_piece, half_piece)
        place = GO.at[pl.ds(at, half_piece), :]
        place[...] = ref[...] * factor
        for i, to in enumerate(holders):
            copy = remote(place, place, f_send.at[p * 3 + i], f_recv.at[p * 3 + i], to)
            copy.start()
            last.append(copy)
    for copy in last:
        copy.wait_recv()
    grad_out = pltpu.make_async_copy(GO, grad, out_sem.at[1])
    grad_out.start()

    for m in range(len(MSGS)):
        message(m).wait_send()
    for copy in [feat_out] + pred_out + res_out + sent + last:
        copy.wait_send()
    resid_out.wait()
    grad_out.wait()


TOTAL_ROWS = [0]


def body(features, targets, centres, widths, coefficients):
    rows, depth = features.shape
    wide = targets.shape[1]
    own = lax.axis_size("own")
    TOTAL_ROWS[0] = rows * own * lax.axis_size("grp")
    unit_rows = (depth // 128 + wide // 128) * PIECE + 8
    cols = UNITS * PIECE
    half = PIECE // 2
    n_loads = 1 + 2 * (depth // 128 + wide // 128)
    vm = pltpu.VMEM
    dma = pltpu.SemaphoreType.DMA
    scratch = [
        vm((UNITS, unit_rows, 128), F32),
        vm((1, widths.shape[0]), F32),
        vm((2, rows, depth), F32),
        vm((2 * rows, depth), BF16),
        vm((2 * rows, 2 * depth), F8),
        vm((2 * rows, 128), F32),
        vm((CHUNK, depth), BF16),
        vm((CHUNK, 2 * depth), F8),
        vm((CHUNK, wide), BF16),
        vm((2 * CHUNK, wide), F8),
        vm((8, CHUNK), F32),
        vm((2 * rows, cols), BF16),
        vm((2 * rows, 2 * cols), F8),
        vm((2 * rows, wide), F32),
        vm((rows, wide), F32),
        vm((rows, wide), F32),
        vm((rows, wide), F32),
        vm((rows, wide), F32),
        vm((wide, 2 * rows), BF16),
        vm((wide, 2 * rows), F8),
        vm((wide, 2 * rows), F8),
        vm((8, wide, CHUNK), F32),
        vm((2, 2, 4, 4, half, wide), F32),
        vm((4, 4, 2, 2, half, wide), F32),
        vm((4 * PIECE, wide), F32),
        vm((2, 2, 4, half, wide), F32),
        vm((2, 4, 4, half, wide), F32),
        vm((2, 2, half, wide), F32),
        vm((2, 4, half, wide), F32),
        vm((2, half // 2, wide), F32),
        vm((2, half, wide), F32),
        vm((2, 2, 2, 2, half, wide), F32),
        vm((2, 4, 2, 2, half, wide), F32),
        vm((2, 2, half, wide), F32),
        vm((2, 2, 2, half, wide), F32),
        vm((2, half // 2, wide), F32),
        vm((2, half, wide), F32),
        dma((n_loads,)), dma((2,)), dma((5,)), dma((5,)), dma((len(MSGS),)), dma((len(MSGS),)),
        dma((24,)), dma((24,)), dma((6,)), dma((6,)), dma((2,)),
    ]
    anywhere = pl.BlockSpec(memory_space=pl.ANY)
    return pl.pallas_call(
        main_kernel,
        out_shape=(
            jax.ShapeDtypeStruct(targets.shape, F32),
            jax.ShapeDtypeStruct(coefficients.shape, F32),
        ),
        in_specs=[anywhere] * 5,
        out_specs=(anywhere, anywhere),
        scratch_shapes=scratch,
        compiler_params=pltpu.CompilerParams(
            collective_id=0, has_side_effects=True, vmem_limit_bytes=67_043_328
        ),
        name="nystrom",
    )(features, targets, centres, widths.reshape(1, -1), coefficients)


def solution(mesh):
    return jax.shard_map(
        body,
        mesh=mesh,
        in_specs=(
            P(("grp", "own"), None),
            P(("grp", "own"), None),
            P("own", None),
            P("own"),
            P("own", None),
        ),
        out_specs=(P(("grp", "own"), None), P("own", None)),
        check_vma=False,
    )
```

time: 461 us -> 97.9 us (0.21)
  waiting for transfers between devices: 257 us -> 0 us
  matrix products: 109 us -> 0 us
  Pallas kernels: 0 us -> 93.3 us
  blocking collectives: 63.2 us -> 0 us
  other arithmetic: 14.8 us -> 0 us
  between operations: 14.1 us -> 0.64 us
    all_gather x1 -> x0, waiting for transfers between devices: 257 us -> none  [side_by_side(): result, at, done = (lax.all_gather(both, axis, axis=dim, tiled=True), 0, [])]
    dot_general x3 -> x0, matrix products: 109 us -> none  [the longest x1 63.6 us: body(): jnp.dot(features, cen_piece.T, precision=lax.Precision.HIGHEST, preferred...]
    pallas_call x0 -> x1, Pallas kernels: none -> 93.3 us  [body(): pl.pallas_call(main_kernel, out_shape=(jax.ShapeDtypeStruct(targets.shape...]
    all_to_all x1 -> x0, blocking collectives: 52.6 us -> none  [sum_at_owner(): lax.all_to_all(parts, axis, split_axis=0, concat_axis=0, tiled=True)]
    reduce_sum x4 -> x0, other arithmetic: 12.6 us -> none  [the longest x1 6.94 us: body(): cen_sq = jnp.sum(cen_piece * cen_piece, axis=1)]
    all_gather x1 -> x0, blocking collectives: 10.6 us -> none  [total_of_pieces(): parts = lax.all_gather(x, axis)]
  transfers between devices with their start and end apart: 1 -> 0, of which waited for: 1 -> 0; matrix products, arithmetic and copies ran while one was open for 1% -> 0% of each run, Pallas kernels for 0% -> 0%
where the time goes in v1:
time: 97.9 us; the launch traced here: 97.8 us
  Pallas kernels  93.3 us (95%)
  local copies, waits for them, and re-layouts  3.83 us (4%)
    pallas_call x1, Pallas kernels, body(): pl.pallas_call(main_kernel, out_shape=(jax.ShapeDtypeStruct(targets.shape...  93.3 us
    unnamed x2, local copies, waits for them, and re-layouts  3.83 us

profile of v1, /device:TPU:1, one launch (start us, length us, event | category | flops | bytes accessed | tf_op | source)
XLA Modules:
  0.0 97.8 jit_solution(13398943389553616762)
XLA Ops:
  0.6 93.3 %nystrom.1 = (f32[1024,256]{1,0:T(8,128)}, f32[128,256]{1,0:T(8,128)}) custom-call(f32[1024,1024]{1,0:T(8,128)} %feat.1, f32[1024,256]{1,0:T(8,128)} %targ.1, f32[128,1024]{1,0:T(8,128)} %cent.1, f32[1,128]{1,0:T(1,128)} %bitcast.1, f32[128,256]{1,0:T(8,128)} %coef.1), custom_call_target="tpu_custom_call" | custom-call | tf_op jit(solution)/shard_map/nystrom/pallas_call | solution.py:556
  93.9 2.3 %copy.9 = f32[1024,256]{1,0:T(8,128)} copy(f32[1024,256]{1,0:T(8,128)} %get-tuple-element.4) | data formatting | bytes 2097152
  96.2 1.6 %copy.10 = f32[128,256]{1,0:T(8,128)} copy(f32[128,256]{1,0:T(8,128)} %get-tuple-element.5) | data formatting | bytes 262144

commit v2 on v1

v2 whole, which is shorter than its diff:
```python
import functools
import math
import jax
import jax.numpy as jnp
from jax import lax
from jax.experimental import pallas as pl
from jax.experimental.pallas import tpu as pltpu
from jax.sharding import PartitionSpec as P

F32, BF16, F8 = jnp.float32, jnp.bfloat16, jnp.float8_e4m3fn
NN = (((1,), (0,)), ((), ()))
NT = (((1,), (1,)), ((), ()))
MESH = pl.DeviceIdType.MESH

PIECE = 32
CHUNK = 256
UNITS = 64
DIRS = ("d1+", "d1-", "d2+", "d2-", "z+", "z-")


def messages():
    out = []

    def add(*m):
        out.append(m)

    for r1 in range(4):
        b = (0, r1, 0)
        if r1 == 0:
            add(0, b, (0, 3, 0), None, "d1+")
            add(0, b, (0, 1, 0), None, "d1-")
        if r1 == 3:
            add(0, b, (0, 2, 0), 0, "d1+")
        if r1 == 1:
            add(0, b, (0, 2, 0), 1, "d1-")
        add(0, b, (0, r1, 3), None, "d2+")
        add(0, b, (0, r1, 1), None, "d2-")
        add(0, (0, r1, 3), (0, r1, 2), 0, "d2+")
        add(0, (0, r1, 1), (0, r1, 2), 1, "d2-")
    for r1 in range(4):
        for r2 in range(4):
            add(0, (0, r1, r2), (1, r1, r2), None, "z+" if (r1 + r2) % 2 == 0 else "z-")
    b = (0, 0, 0)
    add(1, b, (0, 0, 3), None, "d2+")
    add(1, b, (0, 0, 1), None, "d2-")
    add(1, (0, 0, 3), (0, 0, 2), 0, "d2+")
    add(1, (0, 0, 1), (0, 0, 2), 1, "d2-")
    for r2 in range(4):
        add(1, (0, 0, r2), (1, 0, r2), None, "z-" if r2 % 2 == 0 else "z+")
    for rz in range(2):
        for r2 in range(4):
            s = (rz, 0, r2)
            add(1, s, (rz, 3, r2), None, "d1+")
            add(1, s, (rz, 1, r2), None, "d1-")
            add(1, (rz, 3, r2), (rz, 2, r2), 0, "d1+")
            add(1, (rz, 1, r2), (rz, 2, r2), 1, "d1-")
    return out


FIRST = (0, 1, 36, 37, 2, 3, 40, 44, 45, 20)
SCHEDULE = (
    ((0, (15, 16, 17, 32)), (1, (6, 7, 8, 24)), (20, ()), (36, (38, 43, 56, 57)), (37, (39, 41, 48, 49)), (40, (60, 61))),
    (),
    ((2, (4, 23)), (3, (5, 21)), (44, (46,)), (45, (47,))),
    ((6, ()), (15, (11, 12, 28)), (32, ()), (43, (72, 73)), (16, (18, 35))),
    ((17, (19, 33)), (56, (58,)), (57, (59,))),
    ((24, ()), (41, (64, 65)), (7, (9, 27)), (8, (10, 25))),
    ((38, ()), (39, (42, 52, 53))),
    ((48, (50,)), (49, (51,)), (23, ()), (28, ()), (4, ()), (5, (22,))),
    ((60, (62,)), (61, (63,))),
    ((21, ()),),
    ((35, ()), (11, (13, 31)), (12, (14, 29)), (46, ()), (47, ())),
    ((18, ()), (19, (34,)), (33, ()), (42, (68, 69))),
    ((9, ()), (10, (26,))),
    ((72, (74,)), (73, (75,)), (13, ()), (14, (30,)), (58, ()), (59, ())),
    ((27, ()), (31, ()), (64, (66,)), (65, (67,))),
    (),
    ((52, (54,)), (53, (55,)), (25, ())),
    ((50, ()), (51, ()), (29, ()), (62, ()), (63, ())),
    ((68, (70,)), (69, (71,))),
    ((22, ()), (74, ()), (75, ()), (34, ()), (66, ()), (67, ())),
    ((54, ()), (55, ()), (70, ()), (71, ())),
    ((30, ()), (26, ())),
    (),
    (),
)

MSGS = messages()


def unit_order():
    place = {(0, (0, 0, 0)): 0, (1, (0, 0, 0)): 1}
    halves = {}
    for point in SCHEDULE:
        for m, _ in point:
            part, _, dst, half, _ = MSGS[m]
            seen = halves.setdefault((part, dst), set())
            seen.update((0, 1) if half is None else (half,))
            if len(seen) == 2:
                place[(part, dst)] = len(place)
    return place


EARLY = 4
PLACE = unit_order()
UNIT_AT = {v: k for k, v in PLACE.items()}
LOG2E = 1.4426950408889634
S_HI, S_LO = 4.0, 1024.0
S_K, S_KLO = 16.0, 4096.0
S_C, S_CLO = 64.0, 16384.0
S_R, S_RLO = 0.25, 64.0


def dot(a, b, dims):
    return lax.dot_general(a, b, dims, preferred_element_type=F32)


def split(v):
    hi = v.astype(BF16)
    return hi, v - hi.astype(F32)


def main_kernel(
    feat, targ, cent, wid, coef, resid, grad,
    CB, WV, FS, FH, FX, RS, CH, CX, WH, WX, MB, KH, KX, PRED, TG, PR, RES, RP,
    RTH, RTL, RTR, GT, G, GO, A1, B1, A2, B2, ZB,
    in_sem, own_sem, d_send, d_recv, g_send, g_recv, r_send, r_recv, f_send, f_recv, out_sem,
):
    rows, depth = feat.shape
    blocks = depth // 128
    unit_rows = CB.shape[1]
    tile = rows // 2
    wide = TG.shape[1]
    lane_w = wide // 128

    grp, own = lax.axis_index("grp"), lax.axis_index("own")
    core, z_hi = lax.rem(grp, 2), grp // 2
    z, x, y = z_hi * 2 + own // 16, lax.rem(own // 4, 4), lax.rem(own, 4)

    def device(d1=0, d2=0, dz=0, dcore=0):
        nx = lax.rem(x + 4 + d1 * (1 - core) + d2 * core, 4)
        ny = lax.rem(y + 4 + d1 * core + d2 * (1 - core), 4)
        nz = lax.rem(z + 4 + dz, 4)
        nc = lax.rem(core + dcore, 2)
        return ((nz // 2) * 2 + nc, lax.rem(nz, 2) * 16 + nx * 4 + ny)

    near = {
        "d1+": device(d1=1), "d1-": device(d1=-1),
        "d2+": device(d2=1), "d2-": device(d2=-1),
        "z+": device(dz=1), "z-": device(dz=-1),
    }
    sibling = device(dcore=1)
    across = device(dz=2)

    def remote(src, dst, send, recv, to):
        return pltpu.make_async_remote_copy(
            src_ref=src, dst_ref=dst, send_sem=send, recv_sem=recv, device_id=to, device_id_type=MESH
        )

    loads = []

    def load(src, dst):
        copy = pltpu.make_async_copy(src, dst, in_sem.at[len(loads)])
        copy.start()
        loads.append(copy)
        return copy

    load(wid, WV)
    for p in range(2):
        first = pl.multiple_of((core * 2 + p) * PIECE, PIECE)
        for b in range(blocks):
            load(
                cent.at[pl.ds(first, PIECE), pl.ds(b * 128, 128)],
                CB.at[p, pl.ds(b * PIECE, PIECE), :],
            )
        for b in range(lane_w):
            load(
                coef.at[pl.ds(first, PIECE), pl.ds(b * 128, 128)],
                CB.at[p, pl.ds((blocks + b) * PIECE, PIECE), :],
            )
    feat_in = pltpu.make_async_copy(feat, FS.at[0], own_sem.at[0])
    feat_in.start()
    targ_in = pltpu.make_async_copy(targ, TG, own_sem.at[1])
    targ_in.start()

    barrier = pltpu.get_barrier_semaphore()
    peers = list(near.values()) + [sibling, across]
    for to in peers:
        pl.semaphore_signal(barrier, inc=1, device_id=to, device_id_type=MESH)
    for copy in loads:
        copy.wait()

    row_i = lax.broadcasted_iota(jnp.int32, (PIECE, 128), 0)
    lane_i = lax.broadcasted_iota(jnp.int32, (PIECE, 128), 1)
    eye = (row_i == lane_i).astype(F32)
    meta_row = lax.broadcasted_iota(jnp.int32, (8, 128), 0)
    for p in range(2):
        sq = jnp.zeros((PIECE, 128), F32)
        for b in range(blocks):
            v = CB[p, b * PIECE : (b + 1) * PIECE, :]
            sq = sq + v * v
        norm = jnp.sum(sq, axis=1, keepdims=True)
        picked = jnp.where(lane_i == row_i + (core * 2 + p) * PIECE, WV[...], 0.0)
        width = jnp.sum(picked, axis=1, keepdims=True)
        scale = (-0.5 * LOG2E) / width
        norm = jnp.sum(norm * eye, axis=0, keepdims=True)
        scale = jnp.sum(scale * eye, axis=0, keepdims=True)
        CB[p, unit_rows - 8 : unit_rows, :] = jnp.where(
            meta_row == 0, scale, jnp.where(meta_row == 1, norm, 0.0)
        )
    pl.semaphore_wait(barrier, len(peers))

    cut = (unit_rows // 16) * 8
    spans = {None: (0, unit_rows), 0: (0, cut), 1: (cut, unit_rows - cut)}

    def message(m):
        part, src, dst, half, way = MSGS[m]
        at, size = spans[half]
        return remote(
            CB.at[PLACE[(part, src)], pl.ds(at, size), :],
            CB.at[PLACE[(part, dst)], pl.ds(at, size), :],
            g_send.at[m], g_recv.at[m], near[way],
        )

    def service(point):
        for m, onward in point:
            message(m).wait_recv()
            for n in onward:
                message(n).start()

    for m in FIRST:
        message(m).start()
    share = rows // 4
    feat_out = [
        remote(
            feat.at[pl.ds(i * share, share), :], FS.at[1, pl.ds(i * share, share), :],
            d_send.at[i], d_recv.at[i], sibling,
        )
        for i in range(4)
    ]
    for copy in feat_out:
        copy.start()

    def prepare_rows(which, first, count):
        base = which * rows
        step = min(128, count)

        @pl.loop(0, count // step)
        def _(i):
            r = pl.multiple_of(first + i * step, step)
            v = FS[which, pl.ds(r, step), :]
            hi, lo = split(v)
            to = pl.ds(base + r, step)
            FH[to, :] = hi
            FX[to, 0:depth] = (v * S_HI).astype(F8)
            FX[to, depth : 2 * depth] = (lo * S_LO).astype(F8)
            RS[to, :] = jnp.broadcast_to(jnp.sum(v * v, axis=1, keepdims=True), (step, 128))

    def prepare_chunk(k):
        units = range(8 * k, 8 * k + 8)
        for b in range(blocks):
            v = jnp.concatenate([CB[u, b * PIECE : (b + 1) * PIECE, :] for u in units], axis=0)
            hi, lo = split(v)
            CH[:, b * 128 : (b + 1) * 128] = hi
            CX[:, b * 128 : (b + 1) * 128] = (lo * S_LO).astype(F8)
            CX[:, depth + b * 128 : depth + (b + 1) * 128] = (v * S_HI).astype(F8)
        for b in range(lane_w):
            at = (blocks + b) * PIECE
            v = jnp.concatenate([CB[u, at : at + PIECE, :] for u in units], axis=0)
            hi, lo = split(v)
            WH[:, b * 128 : (b + 1) * 128] = hi
            WX[0:CHUNK, b * 128 : (b + 1) * 128] = (lo * S_CLO).astype(F8)
            WX[CHUNK : 2 * CHUNK, b * 128 : (b + 1) * 128] = (v * S_C).astype(F8)
        for h in range(2):
            total = CB[8 * k + 4 * h, unit_rows - 8 : unit_rows, :]
            for j in range(1, 4):
                meta = CB[8 * k + 4 * h + j, unit_rows - 8 : unit_rows, :]
                total = total + pltpu.roll(meta, j * PIECE, 1)
            MB[:, h * 128 : (h + 1) * 128] = total

    def compute(k, base, size):
        r = pl.ds(base, size)
        cross = dot(FH[r, :], CH[...], NT)
        fine = dot(FX[r, :], CX[...], NT)
        norm = RS[r, :]
        norm = jnp.concatenate([norm, norm], axis=1)
        s = (norm + MB[1:2, :]) - 2.0 * cross - fine * (2.0 / (S_HI * S_LO))
        kern = jnp.exp2(s * MB[0:1, :])
        hi, lo = split(kern)
        KH[r, k * CHUNK : (k + 1) * CHUNK] = hi
        both = jnp.concatenate([(kern * S_K).astype(F8), (lo * S_KLO).astype(F8)], axis=1)
        KX[r, 2 * k * CHUNK : 2 * (k + 1) * CHUNK] = both
        term = dot(hi, WH[...], NN) + dot(both, WX[...], NN) * (1.0 / (S_K * S_CLO))
        if k == 0:
            PRED[r, :] = term
        else:
            PRED[r, :] = PRED[r, :] + term

    feat_in.wait()
    prepare_rows(0, 0, rows)
    for i in range(4):
        feat_out[i].wait_recv()
        prepare_rows(1, i * share, share)
    pred_out = [
        remote(
            PRED.at[pl.ds(rows + i * tile, tile), :], PR.at[pl.ds(i * tile, tile), :],
            d_send.at[4 + i], d_recv.at[4 + i], sibling,
        )
        for i in range(2)
    ]
    for k in range(8):
        before, after0, after1 = SCHEDULE[3 * k : 3 * k + 3]
        service(before)
        prepare_chunk(k)
        if k < 7:

            @pl.loop(0, 2)
            def _(s):
                compute(k, pl.multiple_of(s * rows, rows), rows)
                for at, point in ((0, after0), (1, after1)):
                    if point:
                        pl.when(s == at)(functools.partial(service, point))
        else:
            for i in range(2):
                compute(k, rows + i * tile, tile)
                pred_out[i].start()
            service(after0)
            compute(k, 0, rows)
            service(after1)

    def factors(v, at):
        t = v.T
        hi, lo = split(t)
        RTH[:, at : at + tile] = hi
        RTL[:, at : at + tile] = (lo * S_RLO).astype(F8)
        RTR[:, at : at + tile] = (t * S_R).astype(F8)

    targ_in.wait()
    res_out = []
    for i in range(2):
        part = pl.ds(i * tile, tile)
        pred_out[i].wait_recv()
        v = PRED[part, :] + PR[part, :] - TG[part, :]
        RES[part, :] = v
        copy = remote(RES.at[part, :], RP.at[part, :], d_send.at[6 + i], d_recv.at[6 + i], sibling)
        copy.start()
        res_out.append(copy)
        factors(v, i * tile)
    resid_out = pltpu.make_async_copy(RES, resid, out_sem.at[0])
    resid_out.start()

    def gradient_term(base, size, k):
        r = pl.ds(base, size)
        c0, c1, c2 = k * CHUNK, 2 * k * CHUNK, (2 * k + 1) * CHUNK
        term = dot(RTH[:, r], KH[r, c0 : c0 + CHUNK], NN)
        fine = dot(RTL[:, r], KX[r, c1 : c1 + CHUNK], NN) + dot(RTR[:, r], KX[r, c2 : c2 + CHUNK], NN)
        return term + fine * (1.0 / (S_RLO * S_K))

    ways = (("d2", "d1"), ("d1", "d2"))

    def ring_copies(part, level):
        first, second = (A1, B1) if level == 0 else (A2, B2)
        pieces = G.at[part] if level == 0 else G.at[part, 0]
        n = 2 if level == 0 else 1
        up, down = (near[ways[part][level] + sign] for sign in "+-")
        low, high = (pl.ds(0, n), pl.ds(n, n))
        out = []
        for i, (a, span, dst, at, to) in enumerate((
            (2, low, first, None, up), (2, high, first, None, down),
            (1, high, second, high, up), (3, low, second, low, down),
            (1, low, second, low, up), (3, high, second, high, down),
        )):
            side = i % 2
            src = pieces.at[a, span]
            if at is None:
                target = dst.at[part, side] if level == 0 else dst.at[part, pl.ds(side, 1)]
            else:
                target = dst.at[part, side, at]
            sem = part * 12 + level * 6 + i
            out.append((src, target, sem, to))
        return out

    rings = {(p, v): ring_copies(p, v) for p in range(2) for v in range(2)}

    def ring_copy(p, v, i):
        src, target, sem, to = rings[(p, v)][i]
        return remote(src, target, r_send.at[sem], r_recv.at[sem], to)

    def send_unit(part, a, b, rz):
        at = {2: 0 if b < 2 else 1, 1: 2 if b >= 2 else None, 3: 3 if b < 2 else None}.get(a)
        if at is None:
            return
        _, _, sem, to = rings[(part, 0)][at]
        target = A1.at[part, at, b % 2, rz] if a == 2 else B1.at[part, at - 2, b, rz]
        remote(G.at[part, a, b, rz], target, r_send.at[sem], r_recv.at[sem], to).start()

    far = [sum(UNIT_AT[8 * k + j][1][2 - UNIT_AT[8 * k + j][0]] == 2 for j in range(8)) for k in range(8)]
    order = sorted(range(8), key=lambda k: -far[k])
    for i, k in enumerate(order[:EARLY]):
        GT[i] = gradient_term(0, rows, k)
    for i in range(2):
        res_out[i].wait_recv()
        factors(RP[i * tile : (i + 1) * tile, :], rows + i * tile)
    for i, k in enumerate(order):
        t = GT[i] + gradient_term(rows, rows, k) if i < EARLY else gradient_term(0, 2 * rows, k)
        t = t.T
        for j in range(8):
            part, (rz, r1, r2) = UNIT_AT[8 * k + j]
            a, b = (r2, r1) if part == 0 else (r1, r2)
            G[part, a, b, rz] = t[j * PIECE : (j + 1) * PIECE, :]
            send_unit(part, a, b, rz)

    def ring_middle(p, v):
        first = A1 if v == 0 else A2
        n = 2 if v == 0 else 1
        pieces = G.at[p] if v == 0 else G.at[p, 0]
        for side, a, span in ((0, 1, slice(0, n)), (1, 3, slice(n, 2 * n))):
            ring_copy(p, v, side).wait_recv()
            got = first[p, side] if v == 0 else first[p, side : side + 1]
            pieces[a, span] = pieces[a, span] + got
            ring_copy(p, v, 4 + side).start()

    def ring_end(p, v):
        second = B1 if v == 0 else B2
        pieces = G.at[p] if v == 0 else G.at[p, 0]
        for i in range(2, 6):
            ring_copy(p, v, i).wait_recv()
        pieces[0] = pieces[0] + second[p, 0] + second[p, 1]

    ring_middle(0, 0)
    ring_middle(1, 0)
    for p in range(2):
        ring_end(p, 0)
        for i in range(4):
            ring_copy(p, 1, i).start()
    ring_middle(0, 1)
    ring_middle(1, 1)

    z_copies = []
    for p in range(2):
        ring_end(p, 1)
        for i, (rz, to) in enumerate(((0, across), (1, near["z+"]), (1, near["z-"]))):
            copy = remote(G.at[p, 0, 0, rz], ZB.at[i, p], f_send.at[3 * p + i], f_recv.at[3 * p + i], to)
            copy.start()
            z_copies.append(copy)
    factor = 1.0 / math.sqrt(TOTAL_ROWS[0])
    last = []
    for p in range(2):
        for copy in z_copies[3 * p : 3 * p + 3]:
            copy.wait_recv()
        at = pl.multiple_of((core * 2 + p) * PIECE, PIECE)
        place = GO.at[pl.ds(at, PIECE), :]
        place[...] = ((G[p, 0, 0, 0] + ZB[0, p]) + (ZB[1, p] + ZB[2, p])) * factor
        copy = remote(place, place, f_send.at[6 + p], f_recv.at[6 + p], sibling)
        copy.start()
        last.append(copy)
    for copy in last:
        copy.wait_recv()
    grad_out = pltpu.make_async_copy(GO, grad, out_sem.at[1])
    grad_out.start()

    for m in range(len(MSGS)):
        message(m).wait_send()
    for p in range(2):
        for v in range(2):
            for i in range(6):
                ring_copy(p, v, i).wait_send()
    for copy in feat_out + pred_out + res_out + z_copies + last:
        copy.wait_send()
    resid_out.wait()
    grad_out.wait()


TOTAL_ROWS = [0]


def hand_over(res_in, grad_in, res_out, grad_out, held, held_grad, sem_in, sem_out):
    parts = held.shape[0]
    size = held.shape[1]
    pairs = [
        (res_in.at[pl.ds(i * size, size), :], held.at[i], res_out.at[pl.ds(i * size, size), :])
        for i in range(parts)
    ] + [(grad_in, held_grad, grad_out)]
    copies = [pltpu.make_async_copy(a, v, sem_in.at[i]) for i, (a, v, _) in enumerate(pairs)]
    for c in copies:
        c.start()
    backs = [pltpu.make_async_copy(v, b, sem_out.at[i]) for i, (_, v, b) in enumerate(pairs)]
    for c, b in zip(copies, backs):
        c.wait()
        b.start()
    for b in backs:
        b.wait()


def body(features, targets, centres, widths, coefficients):
    rows, depth = features.shape
    wide = targets.shape[1]
    own = lax.axis_size("own")
    TOTAL_ROWS[0] = rows * own * lax.axis_size("grp")
    unit_rows = (depth // 128 + wide // 128) * PIECE + 8
    cols = UNITS * PIECE
    n_loads = 1 + 2 * (depth // 128 + wide // 128)
    vm = pltpu.VMEM
    dma = pltpu.SemaphoreType.DMA
    scratch = [
        vm((UNITS, unit_rows, 128), F32),
        vm((1, widths.shape[0]), F32),
        vm((2, rows, depth), F32),
        vm((2 * rows, depth), BF16),
        vm((2 * rows, 2 * depth), F8),
        vm((2 * rows, 128), F32),
        vm((CHUNK, depth), BF16),
        vm((CHUNK, 2 * depth), F8),
        vm((CHUNK, wide), BF16),
        vm((2 * CHUNK, wide), F8),
        vm((8, CHUNK), F32),
        vm((2 * rows, cols), BF16),
        vm((2 * rows, 2 * cols), F8),
        vm((2 * rows, wide), F32),
        vm((rows, wide), F32),
        vm((rows, wide), F32),
        vm((rows, wide), F32),
        vm((rows, wide), F32),
        vm((wide, 2 * rows), BF16),
        vm((wide, 2 * rows), F8),
        vm((wide, 2 * rows), F8),
        vm((EARLY, wide, CHUNK), F32),
        vm((2, 4, 4, 2, PIECE, wide), F32),
        vm((4 * PIECE, wide), F32),
        vm((2, 2, 2, 2, PIECE, wide), F32),
        vm((2, 2, 4, 2, PIECE, wide), F32),
        vm((2, 2, PIECE, wide), F32),
        vm((2, 2, 2, PIECE, wide), F32),
        vm((3, 2, PIECE, wide), F32),
        dma((n_loads,)), dma((2,)), dma((8,)), dma((8,)), dma((len(MSGS),)), dma((len(MSGS),)),
        dma((24,)), dma((24,)), dma((8,)), dma((8,)), dma((2,)),
    ]
    anywhere = pl.BlockSpec(memory_space=pl.ANY)
    residual, gradient = pl.pallas_call(
        main_kernel,
        out_shape=(
            jax.ShapeDtypeStruct(targets.shape, F32),
            jax.ShapeDtypeStruct(coefficients.shape, F32),
        ),
        in_specs=[anywhere] * 5,
        out_specs=(anywhere, anywhere),
        scratch_shapes=scratch,
        compiler_params=pltpu.CompilerParams(
            collective_id=0, has_side_effects=True, vmem_limit_bytes=67_043_328
        ),
        name="nystrom",
    )(features, targets, centres, widths.reshape(1, -1), coefficients)
    return pl.pallas_call(
        hand_over,
        out_shape=(
            jax.ShapeDtypeStruct(targets.shape, F32),
            jax.ShapeDtypeStruct(coefficients.shape, F32),
        ),
        in_specs=[anywhere] * 2,
        out_specs=(anywhere, anywhere),
        scratch_shapes=[
            vm((4, rows // 4, wide), F32), vm(coefficients.shape, F32), dma((5,)), dma((5,)),
        ],
        name="hand_over",
    )(residual, gradient)


def solution(mesh):
    return jax.shard_map(
        body,
        mesh=mesh,
        in_specs=(
            P(("grp", "own"), None),
            P(("grp", "own"), None),
            P("own", None),
            P("own"),
            P("own", None),
        ),
        out_specs=(P(("grp", "own"), None), P("own", None)),
        check_vma=False,
    )
```

time: 97.9 us -> 88.6 us (0.905)
  Pallas kernels: 93.3 us -> 87.7 us
  local copies, waits for them, and re-layouts: 3.83 us -> 0 us
    pallas_call x1, Pallas kernels: 93.3 us -> 85.7 us  [body(): pl.pallas_call(main_kernel, out_shape=(jax.ShapeDtypeStruct(targets.shape...]
    unnamed x2 -> x0, local copies, waits for them, and re-layouts: 3.83 us -> none
    pallas_call x0 -> x1, Pallas kernels: none -> 2.04 us  [body(): pl.pallas_call(hand_over, out_shape=(jax.ShapeDtypeStruct(targets.shape,...]
where the time goes in v2:
time: 88.6 us; the launch traced here: 88.5 us
  Pallas kernels  87.7 us (99%)
    pallas_call x1, Pallas kernels, body(): pl.pallas_call(main_kernel, out_shape=(jax.ShapeDtypeStruct(targets.shape...  85.7 us
    pallas_call x1, Pallas kernels, body(): pl.pallas_call(hand_over, out_shape=(jax.ShapeDtypeStruct(targets.shape,...  2.04 us

profile of v2, /device:TPU:1, one launch (start us, length us, event | category | flops | bytes accessed | tf_op | source)
XLA Modules:
  0.0 88.5 jit_solution(10159470708960229271)
XLA Ops:
  0.6 85.7 %nystrom.1 = (f32[1024,256]{1,0:T(8,128)}, f32[128,256]{1,0:T(8,128)}) custom-call(f32[1024,1024]{1,0:T(8,128)} %feat.1, f32[1024,256]{1,0:T(8,128)} %targ.1, f32[128,1024]{1,0:T(8,128)} %cent.1, f32[1,128]{1,0:T(1,128)} %bitcast.1, f32[128,256]{1,0:T(8,128)} %coef.1), custom_call_target="tpu_custom_call" | custom-call | tf_op jit(solution)/shard_map/nystrom/pallas_call | solution.py:539
  86.3 2.0 %hand_over.1 = (f32[1024,256]{1,0:T(8,128)}, f32[128,256]{1,0:T(8,128)}) custom-call(f32[1024,256]{1,0:T(8,128)} %get-tuple-element.4.res_in, f32[128,256]{1,0:T(8,128)} %get-tuple-element.5.grad_in), custom_call_target="tpu_custom_call" | custom-call | tf_op jit(solution)/shard_map/hand_over/pallas_call | solution.py:553
